TPU v7x, 8 devices: a whole 2x2x1 slice. The times are simulated.
8 devices in a mesh: dp: 1 (over z), tp: 2 (over y), ep: 4 (over x, core).
Axes of the slice: x: 2, y: 2, z: 1, core: 2. Of those that a mesh axis runs over, the one named last changes fastest.
Arguments:
- normed: bfloat16 [2048, 2048], P(('dp', 'ep'))
- residual: bfloat16 [2048, 2048], P(('dp', 'ep'))
- w_router: float32 [2048, 60], replicated
- ws_gate: bfloat16 [2048, 5632], P(None, 'tp')
- ws_up: bfloat16 [2048, 5632], P(None, 'tp')
- ws_down: bfloat16 [5632, 2048], P('tp')
- we_gate: bfloat16 [60, 2048, 1408], P('ep', None, 'tp')
- we_up: bfloat16 [60, 2048, 1408], P('ep', None, 'tp')
- we_down: bfloat16 [60, 1408, 2048], P('ep', 'tp')
- first_id: int32 [2048], P(('dp', 'ep'))
- alt_id: int32 [2048], P(('dp', 'ep'))
Outputs:
- output: bfloat16 [2048, 2048], P(('dp', 'ep'))
All inputs are finite; a program needn't handle non-finite values.
Results may differ from a plain program's by a relative error of at most 0.00530088.
Values are sent between devices in bfloat16 or wider.
A program may use at most 1 GiB of HBM per device.

v0:
```python
import jax
import jax.numpy as jnp
from jax import lax
from jax.sharding import PartitionSpec as P


def swiglu_rows(token_rows, w_gate, w_up, w_down):
    gate_pre = jnp.dot(token_rows, w_gate, preferred_element_type=jnp.float32)
    up_pre = jnp.dot(token_rows, w_up, preferred_element_type=jnp.float32)
    hidden_act = (jax.nn.silu(gate_pre) * up_pre).astype(jnp.bfloat16)
    return jnp.dot(hidden_act, w_down, preferred_element_type=jnp.float32)


def expert_slots(slot_rows, we_gate, we_up, we_down):
    gate_pre = jnp.einsum('ecd,edf->ecf', slot_rows, we_gate, preferred_element_type=jnp.float32)
    up_pre = jnp.einsum('ecd,edf->ecf', slot_rows, we_up, preferred_element_type=jnp.float32)
    hidden_act = (jax.nn.silu(gate_pre) * up_pre).astype(jnp.bfloat16)
    return jnp.einsum('ecf,efd->ecd', hidden_act, we_down, preferred_element_type=jnp.float32)


def rank_in_column(onehot):
    return jnp.sum(jnp.cumsum(onehot, axis=0) * onehot, axis=1) - 1


def solution(mesh):
    ep_size = mesh.shape['ep']
    tok_spec = P(('dp', 'ep'), None)
    id_spec = P(('dp', 'ep'))

    def device_step(normed, residual, w_router, ws_gate, ws_up, ws_down, we_gate, we_up, we_down, first_id, alt_id):
        tok_count, d_model = normed.shape
        local_experts = we_gate.shape[0]
        experts = local_experts * ep_size
        capacity = (5 * tok_count * ep_size + 4 * experts - 1) // (4 * experts)
        pair_rows = 2 * tok_count // ep_size
        table_size = local_experts * capacity
        recv_count = ep_size * pair_rows
        my_rank = lax.axis_index('ep')
        expert_ids = jnp.arange(experts, dtype=jnp.int32)
        before_me = (jnp.arange(ep_size) < my_rank).astype(jnp.int32)[:, None]

        onehot_first = (first_id[:, None] == expert_ids[None, :]).astype(jnp.int32)
        counts_first = lax.all_gather(jnp.sum(onehot_first, axis=0), 'ep')
        rank_first = jnp.sum(counts_first * before_me, axis=0)[first_id] + rank_in_column(onehot_first)
        kept_mask = rank_first < capacity
        slot_load = jnp.minimum(jnp.sum(counts_first, axis=0), capacity)
        overflow = jnp.logical_not(kept_mask)

        onehot_alt = ((alt_id[:, None] == expert_ids[None, :]) & overflow[:, None]).astype(jnp.int32)
        counts_alt = lax.all_gather(jnp.sum(onehot_alt, axis=0), 'ep')
        rank_alt = jnp.sum(counts_alt * before_me, axis=0)[alt_id] + rank_in_column(onehot_alt)
        recycled = overflow & (rank_alt < (capacity - slot_load)[alt_id])
        active = kept_mask | recycled
        chosen = jnp.where(kept_mask, first_id, alt_id)
        slot_index = jnp.where(kept_mask, rank_first, slot_load[alt_id] + rank_alt)
        owner_rank = chosen // local_experts
        slot_code = (chosen % local_experts) * capacity + slot_index

        onehot_owner = ((owner_rank[:, None] == jnp.arange(ep_size)[None, :]) & active[:, None]).astype(jnp.int32)
        cum_owner = jnp.cumsum(onehot_owner, axis=0)
        pos_owner = jnp.sum(cum_owner * onehot_owner, axis=1) - 1
        targets = jnp.arange(1, pair_rows + 1, dtype=jnp.int32)
        pick_index = jax.vmap(lambda column: jnp.searchsorted(column, targets, side='left'))(cum_owner.T)
        valid_row = (targets[None, :] <= cum_owner[-1][:, None]).reshape(recv_count)
        pick_index = jnp.minimum(pick_index, tok_count - 1).reshape(recv_count)
        send_rows = jnp.take(normed, pick_index, axis=0)
        send_code = jnp.where(valid_row, slot_code[pick_index], -1)
        recv_rows = lax.all_to_all(send_rows, 'ep', 0, 0, tiled=True)
        recv_code = lax.all_to_all(send_code, 'ep', 0, 0, tiled=True)

        slot_source = jnp.full((table_size,), recv_count, jnp.int32).at[jnp.where(recv_code >= 0, recv_code, table_size)].set(jnp.arange(recv_count, dtype=jnp.int32), mode='drop')
        slot_rows = jnp.take(recv_rows, slot_source, axis=0, mode='fill', fill_value=0).reshape(local_experts, capacity, d_model)
        slot_out = lax.psum(expert_slots(slot_rows, we_gate, we_up, we_down), 'tp').astype(jnp.bfloat16).reshape(table_size, d_model)
        back_rows = jnp.take(slot_out, jnp.maximum(recv_code, 0), axis=0)
        ret_rows = lax.all_to_all(back_rows, 'ep', 0, 0, tiled=True)
        routed = jnp.take(ret_rows, jnp.where(active, owner_rank * pair_rows + pos_owner, 0), axis=0)

        router_prob = jax.nn.softmax(jnp.dot(normed, w_router, preferred_element_type=jnp.float32), axis=-1)
        gate_weight = jnp.take_along_axis(router_prob, chosen[:, None], axis=1)[:, 0] * active.astype(jnp.float32)
        shared = lax.psum(swiglu_rows(normed, ws_gate, ws_up, ws_down), 'tp')
        combined = residual.astype(jnp.float32) + shared + gate_weight[:, None] * routed.astype(jnp.float32)
        return combined.astype(jnp.bfloat16)

    return jax.shard_map(device_step, mesh=mesh, in_specs=(tok_spec, tok_spec, P(None, None), P(None, 'tp'), P(None, 'tp'), P('tp', None), P('ep', None, 'tp'), P('ep', None, 'tp'), P('ep', 'tp', None), id_spec, id_spec), out_specs=tok_spec, check_vma=False)
```

profile of v0, /device:TPU:0, one launch (start us, length us, event | category | flops | bytes accessed | tf_op | source)
XLA Modules:
  0.0 707.0 jit_solution(16830115453489925450)
XLA Ops:
  12.3 6.8 all-reduce
  27.0 38.1 %compare_select_fusion.7 = (s32[512]{0:T(512)S(1)}, s32[512]{0:T(512)S(1)}, pred[512]{0:T(512)(128)(4,1)S(1)}, s32[512]{0:T(512)S(1)}) fusion(s32[512]{0:T(512)} %param.22, s32[512]{0:T(512)} %param.23, s32[512]{0:T(512)S(1)} %get-tuple-element.93, s32[]{:T(128)} %bitcast.60, s32[]{:T(128)} %bitcast.59, s32[]{:T(128)} %bitcast.58, s32[]{:T(128)} %bitcast.57, ...), kind=kLoop, calls=%fused_computation.66 | loop fusion | flops 65536 | bytes 13040 | tf_op jit(solution)/shard_map/jit(take_along_axis)/select_n | solution.py:79
  77.0 4.5 gather_fusion.6
  81.5 75.1 %select_select_fusion.2 = (f32[512]{0:T(512)S(1)}, pred[512]{0:T(512)(128)(4,1)S(1)}, pred[512]{0:T(512)(128)(4,1)S(1)}, pred[512]{0:T(512)(128)(4,1)S(1)}, pred...) fusion(f32[512]{0:T(512)S(1)} %gather_fusion.6, ...), kind=kLoop, calls=%fused_computation.99 | loop fusion | flops 99328 | bytes 42464 | tf_op jit(solution)/shard_map/mul | solution.py:79
  158.3 92.5 %while.24 = (s32[]{:T(128)}, u32[4,256]{1,0:T(4,128)S(1)}, u32[4,256]{1,0:T(4,128)S(1)}, s32[4,512]{1,0:T(4,128)S(1)}, s32[]{:T(128)}, /*index=5*/s32[]{:T(128)}) while((s32[]{:T(128)}, u32[4,256]{1,0:T(4,128)S(1)}, u32[4,256]{1,0:T(4,128)S(1)}, s32[4,512]{1,0:T(4,128)S(1)}, s32[]{:T(128)}, /*index=5*/s32[]{:T(128)}) %tuple.338), condition=%wide.region_18.19_spmd.clone, body=%wide.region_17.18_spmd.clone.sunk | while | flops 23811 | bytes 86097 | solution.py:63
  158.4 9.1 %gather_fusion = s32[1024]{0:T(1024)S(1)} fusion(s32[4,512]{1,0:T(4,128)S(1)} %get-tuple-element.467, u32[1024]{0:T(1024)S(1)} %bitcast.330), kind=kCustom, calls=%fused_computation.clone.clone.1 | custom fusion | bytes 16384 | tf_op jit(solution)/shard_map/vmap(jit(searchsorted))/vmap(jit(_searchsorted_scan_impl))/while/body/eval_jaxpr/gather | solution.py:63
  167.6 9.1 %gather_fusion = s32[1024]{0:T(1024)S(1)} fusion(s32[4,512]{1,0:T(4,128)S(1)} %get-tuple-element.467, u32[1024]{0:T(1024)S(1)} %bitcast.330), kind=kCustom, calls=%fused_computation.clone.clone.1 | custom fusion | bytes 16384 | tf_op jit(solution)/shard_map/vmap(jit(searchsorted))/vmap(jit(_searchsorted_scan_impl))/while/body/eval_jaxpr/gather | solution.py:63
  176.9 9.1 %gather_fusion = s32[1024]{0:T(1024)S(1)} fusion(s32[4,512]{1,0:T(4,128)S(1)} %get-tuple-element.467, u32[1024]{0:T(1024)S(1)} %bitcast.330), kind=kCustom, calls=%fused_computation.clone.clone.1 | custom fusion | bytes 16384 | tf_op jit(solution)/shard_map/vmap(jit(searchsorted))/vmap(jit(_searchsorted_scan_impl))/while/body/eval_jaxpr/gather | solution.py:63
  186.1 9.1 %gather_fusion = s32[1024]{0:T(1024)S(1)} fusion(s32[4,512]{1,0:T(4,128)S(1)} %get-tuple-element.467, u32[1024]{0:T(1024)S(1)} %bitcast.330), kind=kCustom, calls=%fused_computation.clone.clone.1 | custom fusion | bytes 16384 | tf_op jit(solution)/shard_map/vmap(jit(searchsorted))/vmap(jit(_searchsorted_scan_impl))/while/body/eval_jaxpr/gather | solution.py:63
  195.4 9.1 %gather_fusion = s32[1024]{0:T(1024)S(1)} fusion(s32[4,512]{1,0:T(4,128)S(1)} %get-tuple-element.467, u32[1024]{0:T(1024)S(1)} %bitcast.330), kind=kCustom, calls=%fused_computation.clone.clone.1 | custom fusion | bytes 16384 | tf_op jit(solution)/shard_map/vmap(jit(searchsorted))/vmap(jit(_searchsorted_scan_impl))/while/body/eval_jaxpr/gather | solution.py:63
  204.6 9.1 %gather_fusion = s32[1024]{0:T(1024)S(1)} fusion(s32[4,512]{1,0:T(4,128)S(1)} %get-tuple-element.467, u32[1024]{0:T(1024)S(1)} %bitcast.330), kind=kCustom, calls=%fused_computation.clone.clone.1 | custom fusion | bytes 16384 | tf_op jit(solution)/shard_map/vmap(jit(searchsorted))/vmap(jit(_searchsorted_scan_impl))/while/body/eval_jaxpr/gather | solution.py:63
  213.9 9.1 %gather_fusion = s32[1024]{0:T(1024)S(1)} fusion(s32[4,512]{1,0:T(4,128)S(1)} %get-tuple-element.467, u32[1024]{0:T(1024)S(1)} %bitcast.330), kind=kCustom, calls=%fused_computation.clone.clone.1 | custom fusion | bytes 16384 | tf_op jit(solution)/shard_map/vmap(jit(searchsorted))/vmap(jit(_searchsorted_scan_impl))/while/body/eval_jaxpr/gather | solution.py:63
  223.1 9.1 %gather_fusion = s32[1024]{0:T(1024)S(1)} fusion(s32[4,512]{1,0:T(4,128)S(1)} %get-tuple-element.467, u32[1024]{0:T(1024)S(1)} %bitcast.330), kind=kCustom, calls=%fused_computation.clone.clone.1 | custom fusion | bytes 16384 | tf_op jit(solution)/shard_map/vmap(jit(searchsorted))/vmap(jit(_searchsorted_scan_impl))/while/body/eval_jaxpr/gather | solution.py:63
  232.4 9.1 %gather_fusion = s32[1024]{0:T(1024)S(1)} fusion(s32[4,512]{1,0:T(4,128)S(1)} %get-tuple-element.467, u32[1024]{0:T(1024)S(1)} %bitcast.330), kind=kCustom, calls=%fused_computation.clone.clone.1 | custom fusion | bytes 16384 | tf_op jit(solution)/shard_map/vmap(jit(searchsorted))/vmap(jit(_searchsorted_scan_impl))/while/body/eval_jaxpr/gather | solution.py:63
  241.6 9.1 %gather_fusion = s32[1024]{0:T(1024)S(1)} fusion(s32[4,512]{1,0:T(4,128)S(1)} %get-tuple-element.467, u32[1024]{0:T(1024)S(1)} %bitcast.330), kind=kCustom, calls=%fused_computation.clone.clone.1 | custom fusion | bytes 16384 | tf_op jit(solution)/shard_map/vmap(jit(searchsorted))/vmap(jit(_searchsorted_scan_impl))/while/body/eval_jaxpr/gather | solution.py:63
  251.0 74.9 %fusion.24 = s32[512]{0:T(512)S(1)} fusion(pred[512]{0:T(512)(128)(4,1)S(1)} %get-tuple-element.170, s32[512]{0:T(512)S(1)} %get-tuple-element.171, pred[512]{0:T(512)(128)(4,1)S(1)} %get-tuple-element.167, pred[512]{0:T(512)(128)(4,1)S(1)} %get-tuple-element.166, pred[512]{0:T(512)(128)(4,1)S(1)} %get-tuple-element.165, ...), kind=kLoop, calls=%fused_computation.81 | loop fusion | flops 66560 | bytes 39392 | tf_op jit(solution)/shard_map/add | solution.py:57
  326.0 6.9 gather_fusion.1
  336.8 6.0 gather_fusion.2
  342.8 11.3 %fusion.57 = f32[512,2816]{1,0:T(8,128)} fusion(bf16[512,2048]{1,0:T(8,128)(2,1)S(1)} %copy-done, bf16[2048,2816]{1,0:T(8,128)(2,1)} %param.16), kind=kOutput, calls=%fused_computation.196 | convolution fusion | flops 5905580032 | bytes 19398656 | tf_op jit(solution)/shard_map/dot_general | solution.py:8
  356.5 4.9 all-to-all-start.1
  361.7 23.4 %fusion.10 = f32[512,2048]{1,0:T(8,128)} fusion(bf16[2816,2048]{1,0:T(8,128)(2,1)} %param.18, f32[512,2816]{1,0:T(8,128)} %fusion.57, bf16[512,2048]{1,0:T(8,128)(2,1)S(1)} %copy-done, bf16[2048,2816]{1,0:T(8,128)(2,1)} %param.17), kind=kOutput, calls=%fused_computation.28 | convolution fusion | flops 11819810816 | bytes 35127296 | tf_op jit(solution)/shard_map/dot_general | solution.py:11
  389.8 19.5 %all-to-all-done.1 = bf16[4,256,2048]{2,1,0:T(8,128)(2,1)} async-done(((bf16[4,256,2048]{2,1,0:T(8,128)(2,1)}), bf16[4,256,2048]{2,1,0:T(8,128)(2,1)}, u32[]{:S(2)}, u32[]{:S(2)}) %all-to-all-start.1) | async-done | bytes 4194336 | tf_op jit(solution)/shard_map/all_to_all | solution.py:68
  409.4 9.7 %gather_fusion.3 = bf16[645,2048]{1,0:T(8,128)(2,1)} fusion(bf16[1024,2048]{1,0:T(8,128)(2,1)} %bitcast.257, s32[1024]{0:T(1024)S(1)} %pad_clamp_fusion.1), kind=kCustom, calls=%fused_computation.3 | custom fusion | bytes 5286420 | tf_op jit(solution)/shard_map/jit(_take)/gather | solution.py:72
  421.3 19.2 %fusion.3 = f32[15,43,704]{2,1,0:T(8,128)} fusion(bf16[15,2048,704]{1,2,0:T(8,128)(2,1)} %param.20, bf16[15,43,2048]{2,1,0:T(8,128)(2,1)S(1)} %gather.62, pred[15,43]{1,0:T(8,128)(4,1)S(1)} %broadcast_in_dim.110), kind=kOutput, calls=%fused_computation.21 | convolution fusion | flops 1861232640 | bytes 47712644 | tf_op jit(solution)/shard_map/ecd,edf->ecf/dot_general | solution.py:16
  440.5 33.0 %fusion.5 = f32[15,43,2048]{2,1,0:T(8,128)} fusion(bf16[15,704,2048]{2,1,0:T(8,128)(2,1)} %param.21, f32[15,43,704]{2,1,0:T(8,128)} %fusion.3, bf16[15,2048,704]{1,2,0:T(8,128)(2,1)} %param.19, bf16[15,43,2048]{2,1,0:T(8,128)(2,1)S(1)} %gather.62, pred[15,43]{1,0:T(8,128)(4,1)S(1)} %broadcast_in_dim.110), kind=kOutput, calls=%fused_computation.24 | convolution fusion | flops 3723869184 | bytes 96250248 | tf_op jit(solution)/shard_map/ecf,efd->ecd/dot_general | solution.py:18
  473.5 147.1 %all-reduce.6 = bf16[15,43,2048]{2,1,0:T(8,128)(2,1)} all-reduce(f32[15,43,2048]{2,1,0:T(8,128)} %fusion.5), channel_id=1, replica_groups=mesh['dp'=1,'tp'=2,'ep'=4] {'tp'}, use_global_device_ids=true, to_apply=%region_20.21 | all-reduce | flops 1320960 | bytes 7925760 | tf_op jit(solution)/shard_map/psum | solution.py:73
  622.9 6.0 gather_fusion.4
  628.9 4.6 broadcast_select_fusion.1
  633.5 5.2 all-to-all-start.2
  638.8 47.5 %all-to-all-done.2 = bf16[4,256,2048]{2,1,0:T(8,128)(2,1)} async-done(((bf16[4,256,2048]{2,1,0:T(8,128)(2,1)}), bf16[4,256,2048]{2,1,0:T(8,128)(2,1)}, u32[]{:S(2)}, u32[]{:S(2)}) %all-to-all-start.2) | async-done | bytes 4194336 | tf_op jit(solution)/shard_map/all_to_all | solution.py:75
  686.3 8.0 %gather_fusion.5 = bf16[512,2048]{1,0:T(8,128)(2,1)} fusion(bf16[1024,2048]{1,0:T(8,128)(2,1)} %bitcast.260, s32[1024]{0:T(1024)S(1)} %pad_clamp_fusion), kind=kCustom, calls=%fused_computation.5 | custom fusion | bytes 4196352 | tf_op jit(solution)/shard_map/jit(_take)/gather | solution.py:76
  694.3 5.9 add_convert_fusion
  (175 shorter events, 43.0 us)
Async XLA Ops:
  6.5 69.5 %copy-start = (bf16[512,2048]{1,0:T(8,128)(2,1)S(1)}, bf16[512,2048]{1,0:T(8,128)(2,1)}, u32[]{:S(2)}) copy-start(bf16[512,2048]{1,0:T(8,128)(2,1)} %param.13) | copy-start | bytes 6291460
  6.5 69.5 %copy-start.3 = (f32[2048,60]{0,1:T(8,128)S(1)}, f32[2048,60]{0,1:T(8,128)}, u32[]{:S(2)}) copy-start(f32[2048,60]{0,1:T(8,128)} %param.15) | copy-start | bytes 1474564
  9.2 72.4 %copy-start.4 = (s32[512]{0:T(512)S(1)}, s32[512]{0:T(512)}, u32[]{:S(2)}) copy-start(s32[512]{0:T(512)} %param.23) | copy-start | bytes 6148
  333.5 23.0 %all-to-all-start = ((s32[4,256,1]{1,2,0:T(1,128)}), s32[4,256,1]{1,2,0:T(1,128)S(1)}, u32[]{:S(2)}, u32[]{:S(2)}) async-start(s32[4,256,1]{1,2,0:T(1,128)} %compare_select_fusion.3), calls=%async_computation | async-start | bytes 8192 | tf_op jit(solution)/shard_map/all_to_all | solution.py:69
  342.8 11.3 %copy-start.2 = (bf16[1024,2048]{1,0:T(8,128)(2,1)S(1)}, bf16[1024,2048]{1,0:T(8,128)(2,1)}, u32[]{:S(2)}) copy-start(bf16[1024,2048]{1,0:T(8,128)(2,1)} %gather_fusion.2) | copy-start | bytes 12582916
  356.5 52.8 %all-to-all-start.1 = ((bf16[4,256,2048]{2,1,0:T(8,128)(2,1)}), bf16[4,256,2048]{2,1,0:T(8,128)(2,1)}, u32[]{:S(2)}, u32[]{:S(2)}) async-start(bf16[4,256,2048]{2,1,0:T(8,128)(2,1)} %broadcast_select_fusion), calls=%async_computation.1 | async-start | bytes 8388608 | tf_op jit(solution)/shard_map/all_to_all | solution.py:68
  361.5 332.8 %all-reduce.5.cloned.1.call-start = ((), (), s32[]{:S(2)}) async-start(), calls=%async_computation.3 | async-start | bytes 8388608 | tf_op jit(solution)/shard_map/psum | solution.py:80
  633.5 52.8 %all-to-all-start.2 = ((bf16[4,256,2048]{2,1,0:T(8,128)(2,1)}), bf16[4,256,2048]{2,1,0:T(8,128)(2,1)}, u32[]{:S(2)}, u32[]{:S(2)}) async-start(bf16[4,256,2048]{2,1,0:T(8,128)(2,1)} %broadcast_select_fusion.1), calls=%async_computation.2 | async-start | bytes 8388608 | tf_op jit(solution)/shard_map/all_to_all | solution.py:75
  694.3 5.9 copy-start.1
Sparse Core Ops, SparseCore 0:
  385.2 112.1 all-reduce.4
where the time goes:
time: 710 us; the launch traced here: 707 us
  other arithmetic  210 us (30%)
  blocking collectives  158 us (22%)
  local copies, waits for them, and re-layouts  155 us (22%)
  matrix products  87.7 us (12%)
  waiting for transfers between devices  67.1 us (9%)
  between operations  14.5 us (2%)
  starting transfers between devices  13.6 us (2%)
    psum x1, blocking collectives, device_step(): lax.psum(expert_slots(slot_rows, we_gate, we_up, we_down), 'tp')  147 us
    gather x10, local copies, waits for them, and re-layouts, device_step(): jnp.searchsorted(column, targets, side='left')  91.3 us
    mul x1, other arithmetic, device_step(): jnp.take_along_axis(router_prob, chosen[:, None], axis=1)[:, 0]  75.1 us
    add x1, other arithmetic, device_step(): slot_code = chosen % local_experts * capacity + slot_index  74.9 us
    all_to_all x1, waiting for transfers between devices, device_step(): ret_rows = lax.all_to_all(back_rows, 'ep', 0, 0, tiled=True)  47.5 us
    select_n x1, other arithmetic, device_step(): jnp.take_along_axis(router_prob, chosen[:, None], axis=1)[:, 0]  38.1 us
    dot_general x1, matrix products, expert_slots(): jnp.einsum('ecf,efd->ecd', hidden_act, we_down, preferred_element_type=jn...  33 us
    dot_general x1, matrix products, swiglu_rows(): return jnp.dot(hidden_act, w_down, preferred_element_type=jnp.float32)  23.4 us
  transfers between devices with their start and end apart: 4, of which 2 were waited for; matrix products, arithmetic and copies ran while one was open for 19% of the time, Pallas kernels for 0%

commit v1 on v0

v1 whole, which is shorter than its diff:
```python
import functools

import jax
import jax.numpy as jnp
from jax import lax
from jax.experimental import pallas as pl
from jax.experimental.pallas import tpu as pltpu
from jax.sharding import PartitionSpec as P

MESH = pl.DeviceIdType.MESH
F32 = jnp.float32
BF16 = jnp.bfloat16
LANES = 128
RANK_BLOCK = 256
X_CHUNKS = 4
OUT_CHUNKS = 4


def dot(a, b):
    return jnp.dot(a, b, preferred_element_type=F32)


def dot_bt(a, b):
    return lax.dot_general(a, b, (((1,), (1,)), ((), ())), preferred_element_type=F32)


def dot_at(a, b):
    return lax.dot_general(a, b, (((0,), (0,)), ((), ())), preferred_element_type=F32)


def moe_kernel(dims, x_hbm, res_hbm, wr_hbm, wsg_hbm, wsu_hbm, wsd_hbm, weg_hbm, weu_hbm, wed_hbm, first_ref, alt_ref, o_hbm,
               x_all, ids_all, code_rows, code_col, gate_col, slot_x, sh_own, sh_send, sh_recv, ex_own, ex_send, ex_recv, ret, out_half, res_half, wr,
               ld_sem, id_send, id_recv, sib_send, sib_recv, xp_send, xp_recv, fw_send, fw_recv,
               ysh_send, ysh_recv, yex_send, yex_recv, rs_send, rs_recv, rx_send, rx_recv, rf_send, rf_recv, yo_send, yo_recv, lo_sem):
    experts, capacity, pad_cap, local_experts, ep_size = dims
    tok, d_model = x_hbm.shape
    half = d_model // 2
    slots = local_experts * pad_cap
    ff_shared = wsg_hbm.shape[1]
    ff_expert = weg_hbm.shape[1]
    dp = lax.axis_index("dp")
    t = lax.axis_index("tp")
    me = lax.axis_index("ep")
    core = lax.rem(me, 2)
    sib = me + 1 - 2 * core
    xp = lax.rem(me + 2, ep_size)
    diag = lax.rem(sib + 2, ep_size)
    y_peer = (dp, 1 - t, me)
    sib_dev = (dp, t, sib)
    xp_dev = (dp, t, xp)
    diag_dev = (dp, t, diag)

    own_x = pltpu.make_async_copy(x_hbm, x_all.at[me], ld_sem.at[0])
    own_x.start()
    own_off = pl.multiple_of(t * half, half)
    peer_off = pl.multiple_of((1 - t) * half, half)
    res_load = pltpu.make_async_copy(res_hbm.at[:, pl.ds(own_off, half)], res_half, ld_sem.at[1])
    res_load.start()
    wr_load = pltpu.make_async_copy(wr_hbm, wr, ld_sem.at[2])
    wr_load.start()

    barrier = pltpu.get_barrier_semaphore()
    for dev in (y_peer, sib_dev, xp_dev, diag_dev):
        pl.semaphore_signal(barrier, inc=1, device_id=dev, device_id_type=MESH)

    ids_all[pl.ds(me, 1), 0:1, :] = first_ref[...].reshape(1, 1, tok)
    ids_all[pl.ds(me, 1), 1:2, :] = alt_ref[...].reshape(1, 1, tok)
    own_x.wait()
    pl.semaphore_wait(barrier, 4)

    def remote(src, dst, s_sem, r_sem, dev):
        return pltpu.make_async_remote_copy(src_ref=src, dst_ref=dst, send_sem=s_sem, recv_sem=r_sem, device_id=dev, device_id_type=MESH)

    id_copies = [remote(ids_all.at[me], ids_all.at[me], id_send.at[i], id_recv.at[i], dev) for i, dev in enumerate((sib_dev, xp_dev, diag_dev))]
    for copy in id_copies:
        copy.start()
    x_rows = tok // X_CHUNKS
    xp_copies = [remote(x_all.at[me, pl.ds(c * x_rows, x_rows)], x_all.at[me, pl.ds(c * x_rows, x_rows)], xp_send.at[c], xp_recv.at[c], xp_dev) for c in range(X_CHUNKS)]
    for copy in xp_copies:
        copy.start()
    sib_copy = remote(x_all.at[me], x_all.at[me], sib_send.at[0], sib_recv.at[0], sib_dev)
    sib_copy.start()
    fw_copies = [remote(x_all.at[xp, pl.ds(c * x_rows, x_rows)], x_all.at[xp, pl.ds(c * x_rows, x_rows)], fw_send.at[c], fw_recv.at[c], sib_dev) for c in range(X_CHUNKS)]

    hc = 256
    n_hidden = ff_shared // hc
    n_half = half // hc

    def ysh_copy(j):
        return remote(sh_send.at[j], sh_recv.at[j], ysh_send.at[j], ysh_recv.at[j], y_peer)

    def shared_phase(act, wg, wu, wd, g_sem, u_sem, d_sem):
        def gate_copy(c, slot):
            return pltpu.make_async_copy(wsg_hbm.at[:, pl.ds(pl.multiple_of(c * hc, hc), hc)], wg.at[slot], g_sem.at[slot])

        def up_copy(c, slot):
            return pltpu.make_async_copy(wsu_hbm.at[:, pl.ds(pl.multiple_of(c * hc, hc), hc)], wu.at[slot], u_sem.at[slot])

        def down_copy(j, slot):
            col = jnp.where(j < n_half, peer_off + j * hc, own_off + (j - n_half) * hc)
            return pltpu.make_async_copy(wsd_hbm.at[:, pl.ds(pl.multiple_of(col, hc), hc)], wd.at[slot], d_sem.at[slot])

        for slot in range(2):
            gate_copy(slot, slot).start()
            up_copy(slot, slot).start()
        for slot in range(2):
            down_copy(slot, slot).start()

        @pl.loop(0, n_hidden)
        def _(c):
            slot = lax.rem(c, 2)
            gate_copy(c, slot).wait()
            up_copy(c, slot).wait()
            x = x_all[me]
            g = dot(x, wg[slot])
            u = dot(x, wu[slot])
            act[:, pl.ds(pl.multiple_of(c * hc, hc), hc)] = (jax.nn.silu(g) * u).astype(BF16)

            @pl.when(c + 2 < n_hidden)
            def _():
                gate_copy(c + 2, slot).start()
                up_copy(c + 2, slot).start()

        @pl.loop(0, n_half)
        def _(j):
            slot = lax.rem(j, 2)
            down_copy(j, slot).wait()
            sh_send[j] = dot(act[...], wd[slot])
            ysh_copy(j).start()
            down_copy(j + 2, slot).start()

        @pl.loop(0, n_half)
        def _(j):
            slot = lax.rem(j, 2)
            down_copy(j + n_half, slot).wait()
            sh_own[j] = dot(act[...], wd[slot])

            @pl.when(j + 2 < n_half)
            def _():
                down_copy(j + n_half + 2, slot).start()

    pl.run_scoped(shared_phase, pltpu.VMEM((tok, ff_shared), BF16), pltpu.VMEM((2, d_model, hc), BF16), pltpu.VMEM((2, d_model, hc), BF16),
                  pltpu.VMEM((2, ff_shared, hc), BF16), pltpu.SemaphoreType.DMA((2,)), pltpu.SemaphoreType.DMA((2,)), pltpu.SemaphoreType.DMA((2,)))

    def yex_copy(e):
        return remote(ex_send.at[e], ex_recv.at[e], yex_send.at[e], yex_recv.at[e], y_peer)

    def routed_phase(sel, wg, wu, wd, g_sem, u_sem, d_sem):
        def gate_copy(e, slot):
            return pltpu.make_async_copy(weg_hbm.at[e], wg.at[slot], g_sem.at[slot])

        def up_copy(e, slot):
            return pltpu.make_async_copy(weu_hbm.at[e], wu.at[slot], u_sem.at[slot])

        def down_copy(e, slot):
            return pltpu.make_async_copy(wed_hbm.at[e], wd.at[slot], d_sem.at[slot])

        for slot in range(2):
            gate_copy(slot, slot).start()
            up_copy(slot, slot).start()
            down_copy(slot, slot).start()

        for copy in id_copies:
            copy.wait()
        e_pad = -(-experts // 8) * 8
        e_iota = lax.broadcasted_iota(jnp.int32, (e_pad, RANK_BLOCK), 0)
        row_i = lax.broadcasted_iota(jnp.int32, (RANK_BLOCK, RANK_BLOCK), 0)
        col_i = lax.broadcasted_iota(jnp.int32, (RANK_BLOCK, RANK_BLOCK), 1)
        upper = (row_i <= col_i).astype(F32).astype(BF16)
        blocks = [(q, b * RANK_BLOCK) for q in range(ep_size) for b in range(tok // RANK_BLOCK)]
        cap = jnp.float32(capacity)
        total = jnp.zeros((e_pad, 1), F32)
        rank_first = []
        for q, lo in blocks:
            first = ids_all[q, 0:1, lo:lo + RANK_BLOCK]
            hot = (e_iota == first).astype(F32)
            cum = dot(hot.astype(BF16), upper) + total
            rank_first.append(jnp.sum(cum * hot, axis=0, keepdims=True) - 1.0)
            total = total + jnp.sum(hot, axis=1, keepdims=True)
        load = jnp.minimum(total, cap)
        room = cap - load
        total = jnp.zeros((e_pad, 1), F32)
        slot_iota = lax.broadcasted_iota(jnp.int32, (slots, RANK_BLOCK), 0).astype(F32)
        base = (me * slots).astype(F32)
        for i, (q, lo) in enumerate(blocks):
            first = ids_all[q, 0:1, lo:lo + RANK_BLOCK]
            alt = ids_all[q, 1:2, lo:lo + RANK_BLOCK]
            kept = rank_first[i] < cap
            over = jnp.where(kept, 0.0, 1.0)
            hot = (e_iota == alt).astype(F32) * over
            cum = dot(hot.astype(BF16), upper) + total
            rank_alt = jnp.sum(cum * hot, axis=0, keepdims=True) - 1.0
            total = total + jnp.sum(hot, axis=1, keepdims=True)
            room_tok = jnp.sum(hot * room, axis=0, keepdims=True)
            load_tok = jnp.sum(hot * load, axis=0, keepdims=True)
            code_first = first.astype(F32) * pad_cap + rank_first[i]
            code_alt = jnp.where(rank_alt < room_tok, alt.astype(F32) * pad_cap + load_tok + rank_alt, -1.0)
            code = jnp.where(kept, code_first, code_alt)
            code_rows[q, :, lo:lo + RANK_BLOCK] = jnp.broadcast_to(code, (8, RANK_BLOCK))
            tok_off = q * tok + lo
            sel[:, tok_off:tok_off + RANK_BLOCK] = (slot_iota == code - base).astype(F32).astype(BF16)

        own_code = jnp.broadcast_to(code_rows[me][0:1, :], (LANES, tok))
        code_t = own_code.T
        code_col[...] = code_t

        wr_load.wait()
        x = x_all[me]
        w = wr[...]
        w_hi = w.astype(BF16)
        w_rest = w - w_hi.astype(F32)
        w_mid = w_rest.astype(BF16)
        w_lo = (w_rest - w_mid.astype(F32)).astype(BF16)
        logits = dot_bt(x, w_hi) + (dot_bt(x, w_mid) + dot_bt(x, w_lo))
        top = jnp.max(logits, axis=1, keepdims=True)
        prob = jnp.exp(logits - top)
        denom = jnp.sum(prob, axis=1, keepdims=True)
        lane_lo = lax.broadcasted_iota(jnp.int32, (tok, experts), 1).astype(F32) * pad_cap
        code_e = code_t[:, 0:experts]
        picked = (code_e >= lane_lo) & (code_e < lane_lo + pad_cap)
        gate = jnp.sum(jnp.where(picked, prob, 0.0), axis=1, keepdims=True) / denom
        gate_col[...] = jnp.broadcast_to(gate, (tok, LANES))

        for c in range(X_CHUNKS):
            xp_copies[c].wait_recv()
            fw_copies[c].start()
        sib_copy.wait()
        for c in range(X_CHUNKS):
            fw_copies[c].wait()
            xp_copies[c].wait_send()

        nc = 256

        @pl.loop(0, d_model // nc)
        def _(n):
            cols = pl.ds(pl.multiple_of(n * nc, nc), nc)
            acc = dot(sel[:, 0:tok], x_all[0, :, cols])
            for q in range(1, ep_size):
                acc = acc + dot(sel[:, q * tok:(q + 1) * tok], x_all[q, :, cols])
            slot_x[:, cols] = acc.astype(BF16)

        @pl.loop(0, local_experts)
        def _(e):
            slot = lax.rem(e, 2)
            gate_copy(e, slot).wait()
            up_copy(e, slot).wait()
            rows = slot_x[pl.ds(pl.multiple_of(e * pad_cap, pad_cap), pad_cap), :]
            g = dot_bt(wg[slot], rows)
            u = dot_bt(wu[slot], rows)
            hidden = (jax.nn.silu(g) * u).astype(BF16)

            @pl.when(e + 2 < local_experts)
            def _():
                gate_copy(e + 2, slot).start()
                up_copy(e + 2, slot).start()

            down_copy(e, slot).wait()
            ex_send[e] = dot_at(hidden, wd[slot, :, pl.ds(peer_off, half)])
            yex_copy(e).start()
            ex_own[e] = dot_at(hidden, wd[slot, :, pl.ds(own_off, half)])

            @pl.when(e + 2 < local_experts)
            def _():
                down_copy(e + 2, slot).start()

    pl.run_scoped(routed_phase, pltpu.VMEM((slots, ep_size * tok), BF16), pltpu.VMEM((2, ff_expert, d_model), BF16), pltpu.VMEM((2, ff_expert, d_model), BF16),
                  pltpu.VMEM((2, ff_expert, d_model), BF16), pltpu.SemaphoreType.DMA((2,)), pltpu.SemaphoreType.DMA((2,)), pltpu.SemaphoreType.DMA((2,)))

    res_load.wait()

    @pl.loop(0, n_half)
    def _(j):
        ysh_copy(j).wait()
        cols = pl.ds(pl.multiple_of(j * hc, hc), hc)
        sh_own[j] = res_half[:, cols].astype(F32) + (sh_own[j] + sh_recv[j])

    def ret_copy(e, who, s_sem, r_sem, dev):
        return remote(ret.at[e, who], ret.at[e, who], s_sem.at[e], r_sem.at[e], dev)

    @pl.loop(0, local_experts)
    def _(e):
        yex_copy(e).wait()
        ret[e, pl.ds(me, 1)] = (ex_own[e] + ex_recv[e]).astype(BF16).reshape(1, pad_cap, half)
        ret_copy(e, me, rx_send, rx_recv, xp_dev).start()
        ret_copy(e, me, rs_send, rs_recv, sib_dev).start()

        def finish(p):
            ret_copy(p, me, rx_send, rx_recv, xp_dev).wait()
            ret_copy(p, xp, rf_send, rf_recv, sib_dev).start()

        @pl.when(e > 0)
        def _():
            finish(e - 1)

        @pl.when(e == local_experts - 1)
        def _():
            finish(e)

    k_lanes = ep_size * pad_cap
    lane = lax.broadcasted_iota(jnp.int32, (tok, k_lanes), 1)
    owner = sum((lane >= q * pad_cap).astype(jnp.int32) for q in range(1, ep_size))
    lane_code = (lane + owner * (slots - pad_cap)).astype(F32)
    code_k = jnp.concatenate([code_col[...]] * 2, axis=1)[:, 0:k_lanes]

    @pl.loop(0, local_experts)
    def _(e):
        ret_copy(e, me, rs_send, rs_recv, sib_dev).wait()
        ret_copy(e, xp, rf_send, rf_recv, sib_dev).wait()
        pick = (code_k == lane_code + (e * pad_cap).astype(F32)).astype(F32).astype(BF16)
        rows = ret[e].reshape(k_lanes, half)
        gate = gate_col[:, 0:1]
        for j in range(n_half):
            sh_own[j] = sh_own[j] + gate * dot(pick, rows[:, j * hc:(j + 1) * hc])

    o_rows = tok // OUT_CHUNKS
    local_outs, y_outs = [], []
    for c in range(OUT_CHUNKS):
        rows = pl.ds(c * o_rows, o_rows)
        for j in range(n_half):
            out_half[rows, j * hc:(j + 1) * hc] = sh_own[j, rows, :].astype(BF16)
        dst = o_hbm.at[rows, pl.ds(own_off, half)]
        copy = remote(out_half.at[rows], dst, yo_send.at[c], yo_recv.at[c], y_peer)
        copy.start()
        y_outs.append(copy)
        copy = pltpu.make_async_copy(out_half.at[rows], dst, lo_sem.at[c])
        copy.start()
        local_outs.append(copy)
    for copy in y_outs + local_outs:
        copy.wait()


def solution(mesh):
    ep_size = mesh.shape["ep"]
    tok_spec = P(("dp", "ep"), None)
    id_spec = P(("dp", "ep"))

    def device_step(normed, residual, w_router, ws_gate, ws_up, ws_down, we_gate, we_up, we_down, first_id, alt_id):
        tok, d_model = normed.shape
        local_experts, _, ff_expert = we_gate.shape
        experts = local_experts * ep_size
        capacity = (5 * tok * ep_size + 4 * experts - 1) // (4 * experts)
        pad_cap = -(-capacity // 16) * 16
        half = d_model // 2
        hc = 256
        slots = local_experts * pad_cap
        dma = pltpu.SemaphoreType.DMA
        any_spec = pl.BlockSpec(memory_space=pl.ANY)
        vmem_spec = pl.BlockSpec(memory_space=pltpu.VMEM)
        return pl.pallas_call(
            functools.partial(moe_kernel, (experts, capacity, pad_cap, local_experts, ep_size)),
            out_shape=jax.ShapeDtypeStruct((tok, d_model), BF16),
            in_specs=[any_spec] * 9 + [vmem_spec] * 2,
            out_specs=any_spec,
            scratch_shapes=[
                pltpu.VMEM((ep_size, tok, d_model), BF16),
                pltpu.VMEM((ep_size, 8, tok), jnp.int32),
                pltpu.VMEM((ep_size, 8, tok), F32),
                pltpu.VMEM((tok, LANES), F32),
                pltpu.VMEM((tok, LANES), F32),
                pltpu.VMEM((slots, d_model), BF16),
                pltpu.VMEM((half // hc, tok, hc), F32),
                pltpu.VMEM((half // hc, tok, hc), F32),
                pltpu.VMEM((half // hc, tok, hc), F32),
                pltpu.VMEM((local_experts, pad_cap, half), F32),
                pltpu.VMEM((local_experts, pad_cap, half), F32),
                pltpu.VMEM((local_experts, pad_cap, half), F32),
                pltpu.VMEM((local_experts, ep_size, pad_cap, half), BF16),
                pltpu.VMEM((tok, half), BF16),
                pltpu.VMEM((tok, half), BF16),
                pltpu.VMEM((experts, d_model), F32),
                dma((3,)), dma((3,)), dma((3,)), dma((1,)), dma((1,)), dma((X_CHUNKS,)), dma((X_CHUNKS,)), dma((X_CHUNKS,)), dma((X_CHUNKS,)),
                dma((half // hc,)), dma((half // hc,)), dma((local_experts,)), dma((local_experts,)),
                dma((local_experts,)), dma((local_experts,)), dma((local_experts,)), dma((local_experts,)), dma((local_experts,)), dma((local_experts,)),
                dma((OUT_CHUNKS,)), dma((OUT_CHUNKS,)), dma((OUT_CHUNKS,)),
            ],
            compiler_params=pltpu.CompilerParams(collective_id=0, has_side_effects=True, vmem_limit_bytes=67043328),
        )(normed, residual, w_router.T, ws_gate, ws_up, ws_down, jnp.swapaxes(we_gate, 1, 2), jnp.swapaxes(we_up, 1, 2), we_down, first_id.reshape(1, tok), alt_id.reshape(1, tok))

    return jax.shard_map(device_step, mesh=mesh, in_specs=(tok_spec, tok_spec, P(None, None), P(None, 'tp'), P(None, 'tp'), P('tp', None), P('ep', None, 'tp'), P('ep', None, 'tp'), P('ep', 'tp', None), id_spec, id_spec), out_specs=tok_spec, check_vma=False)
```

time: 710 us -> 171 us (0.24)
  other arithmetic: 210 us -> 0 us
  Pallas kernels: 0 us -> 167 us
  blocking collectives: 158 us -> 0 us
  local copies, waits for them, and re-layouts: 155 us -> 3.16 us
  matrix products: 87.7 us -> 0 us
  waiting for transfers between devices: 67.1 us -> 0 us
  between operations: 14.5 us -> 0.01 us
  starting transfers between devices: 13.6 us -> 0 us
    pallas_call x0 -> x1, Pallas kernels: none -> 167 us  [device_step(): pl.pallas_call(functools.partial(moe_kernel, (experts, capacity, pad_cap,...]
    psum x1 -> x0, blocking collectives: 147 us -> none  [device_step(): lax.psum(expert_slots(slot_rows, we_gate, we_up, we_down), 'tp')]
    gather x32 -> x0, local copies, waits for them, and re-layouts: 145 us -> none  [the longest x10 91.3 us: device_step(): jnp.searchsorted(column, targets, side='left')]
    dot_general x5 -> x0, matrix products: 87.7 us -> none  [the longest x1 33 us: expert_slots(): jnp.einsum('ecf,efd->ecd', hidden_act, we_down, preferred_element_type=jn...]
    mul x1 -> x0, other arithmetic: 75.1 us -> none  [device_step(): jnp.take_along_axis(router_prob, chosen[:, None], axis=1)[:, 0]]
    add x12 -> x0, other arithmetic: 74.9 us -> none  [the longest x1 74.9 us: device_step(): slot_code = chosen % local_experts * capacity + slot_index]
    all_to_all x3 -> x0, waiting for transfers between devices: 67.1 us -> none  [the longest x1 47.5 us: device_step(): ret_rows = lax.all_to_all(back_rows, 'ep', 0, 0, tiled=True)]
    select_n x27 -> x0, other arithmetic: 46.1 us -> none  [the longest x1 38.1 us: device_step(): jnp.take_along_axis(router_prob, chosen[:, None], axis=1)[:, 0]]
  transfers between devices with their start and end apart: 4 -> 0, of which waited for: 2 -> 0; matrix products, arithmetic and copies ran while one was open for 19% -> 0% of each run, Pallas kernels for 0% -> 0%
where the time goes in v1:
time: 171 us
  Pallas kernels  167 us (98%)
  local copies, waits for them, and re-layouts  3.16 us (2%)
    pallas_call x1, Pallas kernels, device_step(): pl.pallas_call(functools.partial(moe_kernel, (experts, capacity, pad_cap,...  167 us

profile of v1, /device:TPU:0, one launch (start us, length us, event | category | flops | bytes accessed | tf_op | source)
XLA Modules:
  0.0 170.5 jit_solution(16628027256329927108)
XLA Ops:
  0.0 167.4 %shard_map.109 = bf16[512,2048]{1,0:T(8,128)(2,1)} custom-call(bf16[512,2048]{1,0:T(8,128)(2,1)} %x_hbm.1, bf16[512,2048]{1,0:T(8,128)(2,1)} %res_hbm.1, f32[60,2048]{1,0:T(8,128)} %bitcast.7, bf16[2048,2816]{1,0:T(8,128)(2,1)} %wsg_hbm.1, bf16[2048,2816]{1,0:T(8,128)(2,1)} %wsu_hbm.1, bf16[2816,2048]{1,0:T(8,128)(2,1)} %wsd_hbm.1, ...), custom_call_target="tpu_custom_call" | custom-call | tf_op jit(solution)/shard_map/pallas_call | solution.py:349
  167.4 3.2 %copy.13 = bf16[512,2048]{1,0:T(8,128)(2,1)} copy(bf16[512,2048]{1,0:T(8,128)(2,1)} %shard_map.109) | data formatting | bytes 4194304
